TPU v7x, 32 devices: a whole 2x2x4 slice. The times are simulated.
32 devices in a mesh: az: 4 (over y, x), rad: 8 (over z, core).
Axes of the slice: x: 2, y: 2, z: 4, core: 2. Of those that a mesh axis runs over, the one named last changes fastest.
Arguments:
- fields: float32 [5, 96, 32, 512], P(None, 'rad', None, 'az'), may hold values from -6 to 6
- shift: int32 [96], replicated, may hold values from 0 to 511
- fraction: float32 [96], replicated, may hold values from -0.5 to 0.5
- radial_rate: float32 [96, 32], replicated, may hold values from -0.4 to 0.4
Outputs:
- updated: float32 [5, 96, 32, 512], P(None, 'rad', None, 'az')
All inputs are finite; a program needn't handle non-finite values.
Results may differ from a plain program's by a relative error of at most 0.0003.
Values sent between devices are 32-bit elements; how exact they have to be, the bound alone decides.
No kernel may reach another device: no remote copies, remote signals or barrier semaphores. Data moves between devices by JAX's collectives and lax.ppermute only.
A program may use at most 64 MiB of HBM per device.

v0:
```python
import jax
import jax.numpy as jnp
from jax import lax
from jax.sharding import PartitionSpec as P


def with_halo(array, sides, width):
    for axis, dim in sides:
        devices, length = (lax.axis_size(axis), array.shape[dim])
        up = [(i, (i + 1) % devices) for i in range(devices - 1)]
        down = [(j, i) for i, j in up]
        last = lax.slice_in_dim(array, length - width, length, axis=dim)
        first = lax.slice_in_dim(array, 0, width, axis=dim)
        before = lax.ppermute(last, axis, up)
        after = lax.ppermute(first, axis, down)
        array = jnp.concatenate([before, array, after], axis=dim)
    return array


def cut(values, low, count, axis):
    return lax.slice_in_dim(values, low, low + count, axis=axis)


def limited(left, right):
    steep = jnp.minimum(
        jnp.minimum(2.0 * jnp.abs(left), 2.0 * jnp.abs(right)), 0.5 * jnp.abs(left + right)
    )
    return jnp.where(left * right > 0.0, jnp.sign(left) * steep, 0.0)


def flux_change(padded, courant, axis):
    count = padded.shape[axis] - 4
    left = cut(padded, 1, count + 2, axis) - cut(padded, 0, count + 2, axis)
    right = cut(padded, 2, count + 2, axis) - cut(padded, 1, count + 2, axis)
    slope = limited(left, right)
    forward = cut(padded, 1, count + 1, axis) + 0.5 * (1.0 - courant) * cut(
        slope, 0, count + 1, axis
    )
    backward = cut(padded, 2, count + 1, axis) - 0.5 * (1.0 + courant) * cut(
        slope, 1, count + 1, axis
    )
    flux = courant * jnp.where(courant > 0.0, forward, backward)
    return cut(flux, 1, count, axis) - cut(flux, 0, count, axis)


def slice_rows(doubled, starts, length):

    def one_row(row, begin):
        return lax.dynamic_slice_in_dim(row, begin, length, axis=2)

    return jax.vmap(one_row, in_axes=(1, 0), out_axes=1)(doubled, starts)


def shards(fields, shift, fraction, radial_rate):
    rows_here = fields.shape[1]
    start = lax.axis_index("rad") * rows_here
    local_shift = lax.dynamic_slice_in_dim(shift, start, rows_here)
    local_fraction = lax.dynamic_slice_in_dim(fraction, start, rows_here)
    group = lax.axis_size("az")
    per_device = rows_here // group
    offset = lax.axis_index("az") * per_device
    row_shift = lax.dynamic_slice_in_dim(local_shift, offset, per_device)
    row_fraction = lax.dynamic_slice_in_dim(local_fraction, offset, per_device)
    block = lax.all_to_all(fields, "az", split_axis=1, concat_axis=3, tiled=True)
    cycle = block.shape[3]
    doubled = jnp.concatenate([block, block], axis=3)
    rolled = slice_rows(doubled, cycle - row_shift, cycle)
    padded = jnp.concatenate([rolled[:, :, :, -2:], rolled, rolled[:, :, :, :2]], axis=3)
    result = rolled - flux_change(padded, row_fraction[None, :, None, None], 3)
    azimuthal = lax.all_to_all(result, "az", split_axis=3, concat_axis=1, tiled=True)
    edge = jnp.zeros((1, radial_rate.shape[1]), jnp.float32)
    extended = jnp.concatenate([edge, radial_rate[:-1], edge], axis=0)
    face_rates = lax.dynamic_slice_in_dim(extended, start, rows_here + 1)
    ghosted = with_halo(azimuthal, (("rad", 1),), 2)
    return azimuthal - flux_change(ghosted, face_rates[None, :, :, None], 1)


def solution(mesh):
    placed = (P(None, "rad", None, "az"), P(), P(), P())
    return jax.shard_map(
        shards, mesh=mesh, in_specs=placed, out_specs=P(None, "rad", None, "az"), check_vma=False
    )
```

profile of v0, /device:TPU:1, one launch (start us, length us, event | category | flops | bytes accessed | tf_op | source)
XLA Modules:
  0.0 94.6 jit_solution(4504958948228859008)
XLA Ops:
  0.0 2.2 %copy.48 = f32[5,12,32,128]{3,2,0,1:T(8,128)} copy(f32[5,12,32,128]{3,2,1,0:T(8,128)} %param.4) | data formatting | bytes 1966080 | tf_op args[0]
  2.2 4.4 %all-to-all-start = ((f32[5,12,32,128]{3,2,0,1:T(8,128)}), f32[5,12,32,128]{3,2,0,1:T(8,128)S(1)}, u32[]{:S(2)}, u32[]{:S(2)}) async-start(f32[5,12,32,128]{3,2,0,1:T(8,128)} %copy.48), calls=%async_computation | async-start | bytes 1966080 | tf_op jit(solution)/shard_map/all_to_all | solution.py:64
  6.8 12.3 %all-to-all-done = f32[5,12,32,128]{3,2,0,1:T(8,128)S(1)} async-done(((f32[5,12,32,128]{3,2,0,1:T(8,128)}), f32[5,12,32,128]{3,2,0,1:T(8,128)S(1)}, u32[]{:S(2)}, u32[]{:S(2)}) %all-to-all-start) | async-done | bytes 983072 | tf_op jit(solution)/shard_map/all_to_all | solution.py:64
  19.1 0.6 copy.49
  19.7 0.4 all_to_all.29
  20.3 7.0 %copy.50 = f32[5,3,32,1024]{2,0,1,3:T(8,128)} copy(f32[5,3,32,1024]{3,2,1,0:T(8,128)S(1)} %pad_maximum_fusion) | data formatting | bytes 3932160 | tf_op jit(solution)/shard_map/concatenate | solution.py:66
  27.3 8.3 %gather_fusion = f32[3,5,32,512]{2,1,3,0:T(8,128)} fusion(f32[3,5,32,1024]{2,1,0,3:T(8,128)} %bitcast.28, s32[3]{0:T(128)S(1)} %fusion.19), kind=kCustom, calls=%fused_computation | custom fusion | bytes 1966128 | tf_op jit(solution)/shard_map/vmap()/gather | solution.py:49
  35.6 4.0 %copy.51 = f32[3,5,32,512]{3,2,0,1:T(8,128)S(1)} copy(f32[3,5,32,512]{2,1,3,0:T(8,128)} %gather_fusion) | data formatting | bytes 1966080 | tf_op jit(solution)/shard_map/vmap()/gather | solution.py:49
  39.7 1.2 %multiply_select_fusion = f32[5,3,32,514]{3,2,1,0:T(8,128)S(1)} fusion(f32[5,3,32,512]{3,2,1,0:T(8,128)S(1)} %bitcast.22, f32[5,3,32,2]{3,2,1,0:T(8,128)S(1)} %get-tuple-element.9, f32[5,3,32,2]{3,2,1,0:T(8,128)S(1)} %get-tuple-element.10), kind=kLoop, calls=%fused_computation.24 | loop fusion | flops 4934400 | bytes 1977600 | tf_op jit(solution)/shard_map/jit(_where)/select_n | solution.py:28
  40.9 0.9 fusion.3
  42.2 3.5 %copy.52 = f32[5,3,32,512]{2,1,0,3:T(4,128)} copy(f32[5,3,32,512]{3,2,1,0:T(8,128)S(1)} %fusion.17) | data formatting | bytes 1966080 | tf_op jit(solution)/shard_map/sub | solution.py:69
  45.7 5.9 %reshape.29 = f32[4,1,61440]{2,1,0:T(1,128)} reshape(f32[512,5,3,32]{3,2,1,0:T(4,128)} %bitcast.19) | data formatting | bytes 1966080
  51.7 3.8 %all-to-all-start.1 = ((f32[4,1,61440]{2,1,0:T(1,128)}), f32[4,1,61440]{2,1,0:T(1,128)S(1)}, u32[]{:S(2)}, u32[]{:S(2)}) async-start(f32[4,1,61440]{2,1,0:T(1,128)} %reshape.29), calls=%async_computation.1 | async-start | bytes 1966080 | tf_op jit(solution)/shard_map/all_to_all | solution.py:70
  55.7 12.0 %all-to-all-done.1 = f32[4,1,61440]{2,1,0:T(1,128)S(1)} async-done(((f32[4,1,61440]{2,1,0:T(1,128)}), f32[4,1,61440]{2,1,0:T(1,128)S(1)}, u32[]{:S(2)}, u32[]{:S(2)}) %all-to-all-start.1) | async-done | bytes 983072 | tf_op jit(solution)/shard_map/all_to_all | solution.py:70
  67.7 0.5 broadcast.122
  68.2 3.5 %reduce = f32[4,61440]{1,0:T(4,128)S(1)} reduce(f32[4,1,61440]{2,1,0:T(1,128)S(1)} %all-to-all-done.1, f32[]{:T(128)} %broadcast.122), dimensions={1}, to_apply=%all_to_all.30.reduce_sub_computation | reduce | bytes 1966084 | tf_op jit(solution)/shard_map/all_to_all | solution.py:70
  71.7 5.6 %reshape.30 = f32[512,5,3,32]{3,2,1,0:T(4,128)} reshape(f32[4,61440]{1,0:T(4,128)S(1)} %reduce) | data formatting | bytes 1966080
  77.3 3.7 %copy.53 = f32[5,4,3,32,128]{4,3,2,1,0:T(8,128)S(1)} copy(f32[5,4,3,32,128]{3,2,0,4,1:T(4,128)} %bitcast.20) | data formatting | bytes 1966080 | tf_op jit(solution)/shard_map/all_to_all | solution.py:70
  81.1 4.6 %collective-permute-start = (f32[5,2,32,128]{3,2,1,0:T(8,128)S(1)}, f32[5,2,32,128]{3,2,1,0:T(8,128)S(1)}, u32[]{:S(2)}, u32[]{:S(2)}) collective-permute-start(f32[5,2,32,128]{3,2,1,0:T(8,128)S(1)} %get-tuple-element.7), channel_id=1, source_target_pairs={{0,1},{1,2},{2,3},{3,4},{4,5},{5,6},{6,7},{8,9},{9,10},{10,11},{11... | collective-permute-start | bytes 491528 | tf_op jit(solution)/shard_map/ppermute | solution.py:14
  85.7 1.9 %collective-permute-start.1 = (f32[5,2,32,128]{3,2,1,0:T(8,128)S(1)}, f32[5,2,32,128]{3,2,1,0:T(8,128)S(1)}, u32[]{:S(2)}, u32[]{:S(2)}) collective-permute-start(f32[5,2,32,128]{3,2,1,0:T(8,128)S(1)} %get-tuple-element.8), channel_id=1, source_target_pairs={{1,0},{2,1},{3,2},{4,3},{5,4},{6,5},{7,6},{9,8},{10,9},{11,10},{12... | collective-permute-start | bytes 491528 | tf_op jit(solution)/shard_map/ppermute | solution.py:15
  87.9 4.4 %collective-permute-done.1 = f32[5,2,32,128]{3,2,1,0:T(8,128)S(1)} collective-permute-done((f32[5,2,32,128]{3,2,1,0:T(8,128)S(1)}, f32[5,2,32,128]{3,2,1,0:T(8,128)S(1)}, u32[]{:S(2)}, u32[]{:S(2)}) %collective-permute-start.1) | collective-permute-done | bytes 163872 | tf_op jit(solution)/shard_map/ppermute | solution.py:15
  92.3 0.7 multiply_select_fusion.1
  93.0 0.4 fusion.13
  93.4 1.2 %fusion.16 = f32[5,12,32,128]{3,2,1,0:T(8,128)} fusion(f32[5,12,32,128]{3,2,1,0:T(8,128)S(1)} %bitcast.27, f32[5,13,32,128]{3,2,1,0:T(8,128)S(1)} %fusion.13), kind=kLoop, calls=%fused_computation.43 | loop fusion | flops 491520 | bytes 3932160 | tf_op jit(solution)/shard_map/sub | solution.py:75
  (19 shorter events, 1.4 us)
Async XLA Ops:
  2.2 4.4 %copy-start.2 = (s32[96]{0:T(128)S(1)}, s32[96]{0:T(128)}, u32[]{:S(2)}) copy-start(s32[96]{0:T(128)} %param.5) | copy-start | bytes 1156
  2.2 4.5 %copy-start.1 = (f32[96]{0:T(128)S(1)}, f32[96]{0:T(128)}, u32[]{:S(2)}) copy-start(f32[96]{0:T(128)} %param.6) | copy-start | bytes 1156
  2.2 16.8 %all-to-all-start = ((f32[5,12,32,128]{3,2,0,1:T(8,128)}), f32[5,12,32,128]{3,2,0,1:T(8,128)S(1)}, u32[]{:S(2)}, u32[]{:S(2)}) async-start(f32[5,12,32,128]{3,2,0,1:T(8,128)} %copy.48), calls=%async_computation | async-start | bytes 1966080 | tf_op jit(solution)/shard_map/all_to_all | solution.py:64
  51.6 3.8 %copy-start = (f32[96,32]{0,1:T(8,128)S(1)}, f32[96,32]{0,1:T(8,128)}, u32[]{:S(2)}) copy-start(f32[96,32]{0,1:T(8,128)} %param.7) | copy-start | bytes 36868
  51.7 16.1 %all-to-all-start.1 = ((f32[4,1,61440]{2,1,0:T(1,128)}), f32[4,1,61440]{2,1,0:T(1,128)S(1)}, u32[]{:S(2)}, u32[]{:S(2)}) async-start(f32[4,1,61440]{2,1,0:T(1,128)} %reshape.29), calls=%async_computation.1 | async-start | bytes 1966080 | tf_op jit(solution)/shard_map/all_to_all | solution.py:70
  81.1 6.8 %collective-permute-start = (f32[5,2,32,128]{3,2,1,0:T(8,128)S(1)}, f32[5,2,32,128]{3,2,1,0:T(8,128)S(1)}, u32[]{:S(2)}, u32[]{:S(2)}) collective-permute-start(f32[5,2,32,128]{3,2,1,0:T(8,128)S(1)} %get-tuple-element.7), channel_id=1, source_target_pairs={{0,1},{1,2},{2,3},{3,4},{4,5},{5,6},{6,7},{8,9},{9,10},{10,11},{11... | collective-permute-start | bytes 491528 | tf_op jit(solution)/shard_map/ppermute | solution.py:14
  85.7 6.6 %collective-permute-start.1 = (f32[5,2,32,128]{3,2,1,0:T(8,128)S(1)}, f32[5,2,32,128]{3,2,1,0:T(8,128)S(1)}, u32[]{:S(2)}, u32[]{:S(2)}) collective-permute-start(f32[5,2,32,128]{3,2,1,0:T(8,128)S(1)} %get-tuple-element.8), channel_id=1, source_target_pairs={{1,0},{2,1},{3,2},{4,3},{5,4},{6,5},{7,6},{9,8},{10,9},{11,10},{12... | collective-permute-start | bytes 491528 | tf_op jit(solution)/shard_map/ppermute | solution.py:15
where the time goes:
time: 95.2 us; the launch traced here: 94.6 us
  local copies, waits for them, and re-layouts  42.1 us (44%)
  waiting for transfers between devices  29 us (30%)
  starting transfers between devices  14.7 us (15%)
  other arithmetic  8.69 us (9%)
    unnamed x10, local copies, waits for them, and re-layouts  13.9 us
    all_to_all x1, waiting for transfers between devices, shards(): lax.all_to_all(fields, 'az', split_axis=1, concat_axis=3, tiled=True)  12.3 us
    gather x2, local copies, waits for them, and re-layouts, one_row(): return lax.dynamic_slice_in_dim(row, begin, length, axis=2)  12.3 us
    all_to_all x1, waiting for transfers between devices, shards(): lax.all_to_all(result, 'az', split_axis=3, concat_axis=1, tiled=True)  12 us
    concatenate x1, local copies, waits for them, and re-layouts, shards(): doubled = jnp.concatenate([block, block], axis=3)  6.97 us
    ppermute x1, starting transfers between devices, with_halo(): before = lax.ppermute(last, axis, up)  4.57 us
    ppermute x1, waiting for transfers between devices, with_halo(): after = lax.ppermute(first, axis, down)  4.4 us
    all_to_all x1, starting transfers between devices, shards(): lax.all_to_all(fields, 'az', split_axis=1, concat_axis=3, tiled=True)  4.39 us
  transfers between devices with their start and end apart: 4, of which 4 were waited for; matrix products, arithmetic and copies ran while one was open for 0% of the time, Pallas kernels for 0%

commit v1 on v0

v1 whole, which is shorter than its diff:
```python
import functools

import jax
import jax.numpy as jnp
from jax import lax
from jax.experimental import pallas as pl
from jax.experimental.pallas import tpu as pltpu
from jax.sharding import PartitionSpec as P


def pick(table, position):
    chosen = jnp.int32(table[0])
    for place, entry in enumerate(table[1:], 1):
        chosen = jnp.where(position == place, jnp.int32(entry), chosen)
    return chosen


def limited(left, right):
    bound = jnp.where(
        left * right > 0.0, 2.0 * jnp.minimum(jnp.abs(left), jnp.abs(right)), 0.0
    )
    return jnp.maximum(jnp.minimum(0.5 * (left + right), bound), -bound)


def plan(rows, group):
    edges = [0, 1, rows - 2, rows - 1]
    inner = [row for row in range(rows) if row not in edges]
    first = edges + inner[: group - len(edges)]
    rest = inner[group - len(edges):]
    each = len(rest) // group
    starts = [rest[device * each] for device in range(group)] if each else []
    return first, starts, each


def azimuthal_kernel(starts, rows, shift, fraction, *refs):
    group = len(refs) // 2
    parts, results = (refs[:group], refs[group:])
    fields, count, _, width = parts[0].shape
    cycle = group * width
    first = lax.axis_index("rad") * rows + pick(starts, lax.axis_index("az"))
    for step in range(count):
        move = shift[first + step]
        courant = fraction[first + step]
        ahead = courant > 0.0
        weight = jnp.where(ahead, 0.5 * (1.0 - courant), -0.5 * (1.0 + courant))
        late = jnp.where(ahead, move, lax.rem(move + (cycle - 1), cycle))
        for field in range(fields):
            cells = jnp.concatenate(
                [parts[(group - place) % group][field, step] for place in range(group)], axis=1
            )
            right = pltpu.roll(cells, cycle - 1, 1) - cells
            face = cells + weight * limited(pltpu.roll(right, 1, 1), right)
            change = face - pltpu.roll(face, 1, 1)
            final = pltpu.roll(cells, move, 1) - courant * pltpu.roll(change, late, 1)
            for place in range(group):
                results[place][field, step] = final[:, place * width:(place + 1) * width]


def azimuthal(parts, starts, rows, shift, fraction):
    vmem = pl.BlockSpec(memory_space=pltpu.VMEM)
    smem = pl.BlockSpec(memory_space=pltpu.SMEM)
    return pl.pallas_call(
        functools.partial(azimuthal_kernel, starts, rows),
        out_shape=[jax.ShapeDtypeStruct(part.shape, part.dtype) for part in parts],
        in_specs=[smem, smem] + [vmem] * len(parts),
        out_specs=[vmem] * len(parts),
        name="azimuthal",
    )(shift, fraction, *parts)


def radial_kernel(places, rows, rates, *refs):
    parts, result, cells = (refs[:-2], refs[-2], refs[-1])
    here = lax.axis_index("az")
    for part, place in zip(parts, places):
        start = pick(place, here)
        for step in range(part.shape[1]):
            cells[start + step] = part[0, step]
    before, middle = (cells[0], cells[1])
    left = middle - before
    slope_before = cell_before = flux_before = None
    for row in range(rows + 2):
        after = cells[row + 2]
        right = after - middle
        slope = limited(left, right)
        if row:
            courant = rates[row - 1]
            forward = cell_before + 0.5 * (1.0 - courant) * slope_before
            backward = middle - 0.5 * (1.0 + courant) * slope
            flux = courant * jnp.where(courant > 0.0, forward, backward)
            if row > 1:
                result[0, row - 2] = cell_before - (flux - flux_before)
            flux_before = flux
        slope_before, cell_before, middle, left = (slope, middle, after, right)


def radial(parts, places, rates, rows):
    fields, _, polar, width = parts[0].shape
    spec = lambda count: pl.BlockSpec((1, count, polar, width), lambda field: (field, 0, 0, 0))
    return pl.pallas_call(
        functools.partial(radial_kernel, places, rows),
        grid=(fields,),
        out_shape=jax.ShapeDtypeStruct((fields, rows, polar, width), jnp.float32),
        in_specs=[pl.BlockSpec(rates.shape, lambda field: (0, 0, 0))]
        + [spec(part.shape[1]) for part in parts],
        out_specs=spec(rows),
        scratch_shapes=[pltpu.VMEM((rows + 5, polar, width), jnp.float32)],
        name="radial",
    )(rates, *parts)


def exchange(parts, group):
    moved = [
        lax.ppermute(part, "az", [(i, (i + k) % group) for i in range(group)])
        for k, part in enumerate(parts[1:], 1)
    ]
    return [parts[0]] + moved


def shards(fields, shift, fraction, radial_rate):
    rows, width = (fields.shape[1], fields.shape[3])
    group, blocks = (lax.axis_size("az"), lax.axis_size("rad"))
    here = lax.axis_index("az")
    first, starts, each = plan(rows, group)
    sets = [(first, 1)] + ([(starts, each)] if each else [])

    def cut_for(place, table, count):
        row = jnp.asarray(table, jnp.int32)[(here + place) % group]
        return lax.dynamic_slice_in_dim(fields, row, count, axis=1)

    cycles = [
        exchange([cut_for(k, table, count) for k in range(group)], group) for table, count in sets
    ]
    parts, places = ([], [])
    for (table, count), cycle in zip(sets, cycles):
        updated = exchange(azimuthal(cycle, table, rows, shift, fraction), group)
        for k in range(group):
            parts.append(updated[k])
            places.append([2 + table[(i - k) % group] for i in range(group)])
    for k in range(group):
        pairs, place = ([], [])
        for i in range(group):
            row = first[(i - k) % group]
            step = -1 if row < 2 else 1 if row >= rows - 2 else 0
            place.append({-1: rows + 2 + row, 1: row - (rows - 2), 0: rows + 4}[step])
            if step:
                pairs += [
                    (i * blocks + b, i * blocks + b + step)
                    for b in range(blocks)
                    if 0 <= b + step < blocks
                ]
        parts.append(lax.ppermute(parts[k], ("az", "rad"), pairs))
        places.append(place)
    edge = jnp.zeros((1, radial_rate.shape[1]), jnp.float32)
    extended = jnp.concatenate([edge, radial_rate[:-1], edge], axis=0)
    face_rates = lax.dynamic_slice_in_dim(extended, lax.axis_index("rad") * rows, rows + 1)
    rates = jnp.broadcast_to(face_rates[:, :, None], face_rates.shape + (width,))
    return radial(parts, places, rates, rows)


def solution(mesh):
    placed = (P(None, "rad", None, "az"), P(), P(), P())
    return jax.shard_map(
        shards, mesh=mesh, in_specs=placed, out_specs=P(None, "rad", None, "az"), check_vma=False
    )
```

time: 95.2 us -> 69 us (0.72)
  local copies, waits for them, and re-layouts: 42.1 us -> 7.17 us
  waiting for transfers between devices: 29 us -> 5.5 us
  between operations: 0.15 us -> 15.3 us
  starting transfers between devices: 14.7 us -> 28.6 us
  Pallas kernels: 0 us -> 11.5 us
  other arithmetic: 8.69 us -> 0.09 us
    all_to_all x2 -> x0, waiting for transfers between devices: 24.3 us -> none  [the longest x1 12.3 us: shards(): lax.all_to_all(fields, 'az', split_axis=1, concat_axis=3, tiled=True)]
    ppermute x2 -> x16, starting transfers between devices: 6.49 us -> 28.6 us  [the longest x12 14.5 us: exchange(): lax.ppermute(part, 'az', [(i, (i + k) % group) for i in range(group)])]
    gather x2 -> x0, local copies, waits for them, and re-layouts: 12.3 us -> none  [one_row(): return lax.dynamic_slice_in_dim(row, begin, length, axis=2)]
    unnamed x10 -> x38, local copies, waits for them, and re-layouts: 13.9 us -> 1.98 us
    pallas_call x0 -> x3, Pallas kernels: none -> 11.5 us  [the longest x2 7 us: azimuthal(): pl.pallas_call(functools.partial(azimuthal_kernel, starts, rows), out_sha...]
    all_to_all x2 -> x0, starting transfers between devices: 8.21 us -> none  [the longest x1 4.39 us: shards(): lax.all_to_all(fields, 'az', split_axis=1, concat_axis=3, tiled=True)]
    concatenate x1 -> x0, local copies, waits for them, and re-layouts: 6.97 us -> none  [shards(): doubled = jnp.concatenate([block, block], axis=3)]
    all_to_all x4 -> x0, local copies, waits for them, and re-layouts: 5.27 us -> none  [the longest x2 4.23 us: shards(): lax.all_to_all(result, 'az', split_axis=3, concat_axis=1, tiled=True)]
  transfers between devices with their start and end apart: 4 -> 16, of which waited for: 4 -> 2; matrix products, arithmetic and copies ran while one was open for 0% -> 3% of each run, Pallas kernels for 0% -> 10%
where the time goes in v1:
time: 69 us; the launch traced here: 68.2 us
  starting transfers between devices  28.6 us (41%)
  between operations  15.3 us (22%)
  Pallas kernels  11.5 us (17%)
  local copies, waits for them, and re-layouts  7.17 us (10%)
  waiting for transfers between devices  5.5 us (8%)
    ppermute x12, starting transfers between devices, exchange(): lax.ppermute(part, 'az', [(i, (i + k) % group) for i in range(group)])  14.5 us
    ppermute x4, starting transfers between devices, shards(): parts.append(lax.ppermute(parts[k], ('az', 'rad'), pairs))  14.1 us
    pallas_call x2, Pallas kernels, azimuthal(): pl.pallas_call(functools.partial(azimuthal_kernel, starts, rows), out_sha...  7 us
    pallas_call x1, Pallas kernels, radial(): pl.pallas_call(functools.partial(radial_kernel, places, rows), grid=(fiel...  4.51 us
    ppermute x4, waiting for transfers between devices, shards(): parts.append(lax.ppermute(parts[k], ('az', 'rad'), pairs))  3.64 us
    dynamic_slice x2, local copies, waits for them, and re-layouts, cut_for(): return lax.dynamic_slice_in_dim(fields, row, count, axis=1)  3.57 us
    unnamed x38, local copies, waits for them, and re-layouts  1.98 us
    ppermute x12, waiting for transfers between devices, exchange(): lax.ppermute(part, 'az', [(i, (i + k) % group) for i in range(group)])  1.86 us
  transfers between devices with their start and end apart: 16, of which 2 were waited for; matrix products, arithmetic and copies ran while one was open for 3% of the time, Pallas kernels for 10%

profile of v1, /device:TPU:1, one launch (start us, length us, event | category | flops | bytes accessed | tf_op | source)
XLA Modules:
  0.0 68.2 jit_solution(13423150491980080598)
XLA Ops:
  0.0 0.7 copy-done.17
  0.7 0.7 fusion
  8.8 1.7 %constant_dynamic-slice_fusion.4 = (f32[5,1,32,128]{3,2,1,0:T(8,128)S(1)}, f32[5,1,32,128]{3,2,1,0:T(8,128)S(1)}, f32[5,1,32,128]{3,2,1,0:T(8,128)S(1)}, f32[5,1,32,128]{3,2,1,0:T(8,128)}) fusion(f32[5,12,32,128]{3,2,1,0:T(8,128)} %param.12, s32[]{:T(128)S(6)} %select_n.82, s32[]{:T(128)S(6)} %select_n.79, s32[]{:T(128)S(6)} %select_n.76, s32[]{:T(128)S(6)} %select_n.73), kind=kLoop, calls=%fused_computation.6 | loop fusion | bytes 655376 | tf_op jit(solution)/shard_map/dynamic_slice | solution.py:128
  10.5 3.0 %collective-permute-start.2 = (f32[5,1,32,128]{3,2,1,0:T(8,128)S(1)}, f32[5,1,32,128]{3,2,1,0:T(8,128)S(1)}, u32[]{:S(2)}, u32[]{:S(2)}) collective-permute-start(f32[5,1,32,128]{3,2,1,0:T(8,128)S(1)} %get-tuple-element.25), channel_id=1, source_target_pairs={{0,24},{8,0},{16,8},{24,16},{1,25},{9,1},{17,9},{25,17},{2,26},{10... | collective-permute-start | bytes 245768 | tf_op jit(solution)/shard_map/ppermute | solution.py:113
  13.7 0.3 collective-permute-start
  21.6 1.9 %constant_dynamic-slice_fusion = (f32[5,2,32,128]{3,2,1,0:T(8,128)S(1)}, f32[5,2,32,128]{3,2,1,0:T(8,128)S(1)}, f32[5,2,32,128]{3,2,1,0:T(8,128)}, f32[5,2,32,128]{3,2,1,0:T(8,128)S(1)}) fusion(f32[5,12,32,128]{3,2,1,0:T(8,128)} %param.12, s32[]{:T(128)S(6)} %select_n.86, s32[]{:T(128)S(6)} %select_n.84, s32[]{:T(128)S(6)} %select_n.83, s32[]{:T(128)S(6)} %select_n.85), kind=kLoop, calls=%fused_computation.2 | loop fusion | bytes 1310736 | tf_op jit(solution)/shard_map/dynamic_slice | solution.py:128
  23.5 2.1 %collective-permute-start.8 = (f32[5,2,32,128]{3,2,1,0:T(8,128)S(1)}, f32[5,2,32,128]{3,2,1,0:T(8,128)S(1)}, u32[]{:S(2)}, u32[]{:S(2)}) collective-permute-start(f32[5,2,32,128]{3,2,1,0:T(8,128)S(1)} %get-tuple-element.21), channel_id=1, source_target_pairs={{0,24},{8,0},{16,8},{24,16},{1,25},{9,1},{17,9},{25,17},{2,26},{10... | collective-permute-start | bytes 491528 | tf_op jit(solution)/shard_map/ppermute | solution.py:113
  25.6 1.2 %collective-permute-start.7 = (f32[5,2,32,128]{3,2,1,0:T(8,128)S(1)}, f32[5,2,32,128]{3,2,1,0:T(8,128)S(1)}, u32[]{:S(2)}, u32[]{:S(2)}) collective-permute-start(f32[5,2,32,128]{3,2,1,0:T(8,128)S(1)} %get-tuple-element.24), channel_id=1, source_target_pairs={{0,16},{8,24},{16,0},{24,8},{1,17},{9,25},{17,1},{25,9},{2,18},{10... | collective-permute-start | bytes 491528 | tf_op jit(solution)/shard_map/ppermute | solution.py:113
  26.9 0.6 copy-done.14
  27.5 2.7 %azimuthal.2 = (f32[5,1,32,128]{3,2,1,0:T(8,128)}, f32[5,1,32,128]{3,2,1,0:T(8,128)}, f32[5,1,32,128]{3,2,1,0:T(8,128)}, f32[5,1,32,128]{3,2,1,0:T(8,128)}) custom-call(s32[96]{0:T(128)} %shift.3, f32[96]{0:T(128)} %fraction.3, f32[5,1,32,128]{3,2,1,0:T(8,128)} %get-tuple-element.28.refs_0_, f32[5,1,32,128]{3,2,1,0:T(8,128)} %copy-done.15, ...), custom_call_target="tpu_custom_call" | custom-call | tf_op jit(solution)/shard_map/azimuthal/pallas_call | solution.py:62
  30.2 1.3 %collective-permute-start.3 = (f32[5,1,32,128]{3,2,1,0:T(8,128)}, f32[5,1,32,128]{3,2,1,0:T(8,128)S(1)}, u32[]{:S(2)}, u32[]{:S(2)}) collective-permute-start(f32[5,1,32,128]{3,2,1,0:T(8,128)} %get-tuple-element.14), channel_id=1, source_target_pairs={{0,8},{8,16},{16,24},{24,0},{1,9},{9,17},{17,25},{25,1},{2,10},{10... | collective-permute-start | bytes 245768 | tf_op jit(solution)/shard_map/ppermute | solution.py:113
  31.6 1.2 %collective-permute-start.4 = (f32[5,1,32,128]{3,2,1,0:T(8,128)}, f32[5,1,32,128]{3,2,1,0:T(8,128)S(1)}, u32[]{:S(2)}, u32[]{:S(2)}) collective-permute-start(f32[5,1,32,128]{3,2,1,0:T(8,128)} %get-tuple-element.15), channel_id=1, source_target_pairs={{0,16},{8,24},{16,0},{24,8},{1,17},{9,25},{17,1},{25,9},{2,18},{10... | collective-permute-start | bytes 245768 | tf_op jit(solution)/shard_map/ppermute | solution.py:113
  32.8 1.8 %collective-permute-done.3.refs_1_ = f32[5,1,32,128]{3,2,1,0:T(8,128)S(1)} collective-permute-done((f32[5,1,32,128]{3,2,1,0:T(8,128)}, f32[5,1,32,128]{3,2,1,0:T(8,128)S(1)}, u32[]{:S(2)}, u32[]{:S(2)}) %collective-permute-start.3) | collective-permute-done | bytes 81952 | tf_op jit(solution)/shard_map/ppermute | solution.py:113
  34.6 2.4 %collective-permute-start.5 = (f32[5,1,32,128]{3,2,1,0:T(8,128)}, f32[5,1,32,128]{3,2,1,0:T(8,128)S(1)}, u32[]{:S(2)}, u32[]{:S(2)}) collective-permute-start(f32[5,1,32,128]{3,2,1,0:T(8,128)} %get-tuple-element.16), channel_id=1, source_target_pairs={{0,24},{8,0},{16,8},{24,16},{1,25},{9,1},{17,9},{25,17},{2,26},{10... | collective-permute-start | bytes 245768 | tf_op jit(solution)/shard_map/ppermute | solution.py:113
  37.1 4.6 %collective-permute-start.12 = (f32[5,1,32,128]{3,2,1,0:T(8,128)}, f32[5,1,32,128]{3,2,1,0:T(8,128)S(1)}, u32[]{:S(2)}, u32[]{:S(2)}) collective-permute-start(f32[5,1,32,128]{3,2,1,0:T(8,128)} %get-tuple-element.13.refs_0_), channel_id=1, source_target_pairs={{1,0},{2,1},{3,2},{4,3},{5,4},{6,5},{7,6},{9,8},{10,9},{11,10},{12... | collective-permute-start | bytes 245768 | tf_op jit(solution)/shard_map/ppermute | solution.py:151
  41.7 3.1 %collective-permute-start.13 = (f32[5,1,32,128]{3,2,1,0:T(8,128)S(1)}, f32[5,1,32,128]{3,2,1,0:T(8,128)S(1)}, u32[]{:S(2)}, u32[]{:S(2)}) collective-permute-start(f32[5,1,32,128]{3,2,1,0:T(8,128)S(1)} %collective-permute-done.3.refs_1_), channel_id=1, source_target_pairs={{0,1},{1,2},{2,3},{3,4},{4,5},{5,6},{6,7},{9,8},{10,9},{11,10},{12... | collective-permute-start | bytes 245768 | tf_op jit(solution)/shard_map/ppermute | solution.py:151
  44.9 0.6 copy-done.5
  45.5 4.3 %azimuthal.3 = (f32[5,2,32,128]{3,2,1,0:T(8,128)}, f32[5,2,32,128]{3,2,1,0:T(8,128)}, f32[5,2,32,128]{3,2,1,0:T(8,128)}, f32[5,2,32,128]{3,2,1,0:T(8,128)}) custom-call(s32[96]{0:T(128)} %shift.3, f32[96]{0:T(128)} %fraction.3, f32[5,2,32,128]{3,2,1,0:T(8,128)} %get-tuple-element.23.refs_0_, f32[5,2,32,128]{3,2,1,0:T(8,128)} %copy-done.4, ...), custom_call_target="tpu_custom_call" | custom-call | tf_op jit(solution)/shard_map/azimuthal/pallas_call | solution.py:62
  50.2 2.3 %collective-permute-start.11 = (f32[5,2,32,128]{3,2,1,0:T(8,128)}, f32[5,2,32,128]{3,2,1,0:T(8,128)S(1)}, u32[]{:S(2)}, u32[]{:S(2)}) collective-permute-start(f32[5,2,32,128]{3,2,1,0:T(8,128)} %get-tuple-element.20), channel_id=1, source_target_pairs={{0,24},{8,0},{16,8},{24,16},{1,25},{9,1},{17,9},{25,17},{2,26},{10... | collective-permute-start | bytes 491528 | tf_op jit(solution)/shard_map/ppermute | solution.py:113
  52.4 4.5 %collective-permute-start.14 = (f32[5,1,32,128]{3,2,1,0:T(8,128)S(1)}, f32[5,1,32,128]{3,2,1,0:T(8,128)S(1)}, u32[]{:S(2)}, u32[]{:S(2)}) collective-permute-start(f32[5,1,32,128]{3,2,1,0:T(8,128)S(1)} %collective-permute-done.4.refs_2_), channel_id=1, source_target_pairs={{0,1},{1,2},{2,3},{3,4},{4,5},{5,6},{6,7},{8,9},{9,10},{10,11},{11... | collective-permute-start | bytes 245768 | tf_op jit(solution)/shard_map/ppermute | solution.py:151
  56.9 1.9 %collective-permute-start.15 = (f32[5,1,32,128]{3,2,1,0:T(8,128)S(1)}, f32[5,1,32,128]{3,2,1,0:T(8,128)S(1)}, u32[]{:S(2)}, u32[]{:S(2)}) collective-permute-start(f32[5,1,32,128]{3,2,1,0:T(8,128)S(1)} %collective-permute-done.5.refs_3_), channel_id=1, source_target_pairs={{1,0},{2,1},{3,2},{4,3},{5,4},{6,5},{7,6},{8,9},{9,10},{10,11},{11... | collective-permute-start | bytes 245768 | tf_op jit(solution)/shard_map/ppermute | solution.py:151
  59.1 3.6 %collective-permute-done.15.refs_11_ = f32[5,1,32,128]{3,2,1,0:T(8,128)S(1)} collective-permute-done((f32[5,1,32,128]{3,2,1,0:T(8,128)S(1)}, f32[5,1,32,128]{3,2,1,0:T(8,128)S(1)}, u32[]{:S(2)}, u32[]{:S(2)}) %collective-permute-start.15) | collective-permute-done | bytes 81952 | tf_op jit(solution)/shard_map/ppermute | solution.py:151
  62.7 0.9 %broadcast_in_dim.10.rates = f32[13,32,128]{2,1,0:T(8,128)} broadcast(f32[13,32]{1,0:T(8,128)S(1)} %copy.13), dimensions={0,1} | broadcast | bytes 214656 | tf_op jit(solution)/shard_map/broadcast_in_dim | solution.py:156
  63.7 4.5 %radial.1 = f32[5,12,32,128]{3,2,1,0:T(8,128)} custom-call(f32[13,32,128]{2,1,0:T(8,128)} %broadcast_in_dim.10.rates, f32[5,1,32,128]{3,2,1,0:T(8,128)} %get-tuple-element.13.refs_0_, f32[5,1,32,128]{3,2,1,0:T(8,128)} %copy-done.6, f32[5,1,32,128]{3,2,1,0:T(8,128)} %copy-done.7, f32[5,1,32,128]{3,2,1,0:T(8,128)} %copy-done.8, ...), custom_call_target="tpu_custom_call" | custom-call | tf_op jit(solution)/shard_map/radial/pallas_call | solution.py:99
  (56 shorter events, 0.9 us)
Async XLA Ops:
  10.5 15.1 %collective-permute-start.2 = (f32[5,1,32,128]{3,2,1,0:T(8,128)S(1)}, f32[5,1,32,128]{3,2,1,0:T(8,128)S(1)}, u32[]{:S(2)}, u32[]{:S(2)}) collective-permute-start(f32[5,1,32,128]{3,2,1,0:T(8,128)S(1)} %get-tuple-element.25), channel_id=1, source_target_pairs={{0,24},{8,0},{16,8},{24,16},{1,25},{9,1},{17,9},{25,17},{2,26},{10... | collective-permute-start | bytes 245768 | tf_op jit(solution)/shard_map/ppermute | solution.py:113
  13.5 13.4 %collective-permute-start.1 = (f32[5,1,32,128]{3,2,1,0:T(8,128)S(1)}, f32[5,1,32,128]{3,2,1,0:T(8,128)S(1)}, u32[]{:S(2)}, u32[]{:S(2)}) collective-permute-start(f32[5,1,32,128]{3,2,1,0:T(8,128)S(1)} %get-tuple-element.26), channel_id=1, source_target_pairs={{0,16},{8,24},{16,0},{24,8},{1,17},{9,25},{17,1},{25,9},{2,18},{10... | collective-permute-start | bytes 245768 | tf_op jit(solution)/shard_map/ppermute | solution.py:113
  13.7 13.2 %collective-permute-start = (f32[5,1,32,128]{3,2,1,0:T(8,128)S(1)}, f32[5,1,32,128]{3,2,1,0:T(8,128)S(1)}, u32[]{:S(2)}, u32[]{:S(2)}) collective-permute-start(f32[5,1,32,128]{3,2,1,0:T(8,128)S(1)} %get-tuple-element.27), channel_id=1, source_target_pairs={{0,8},{8,16},{16,24},{24,0},{1,9},{9,17},{17,25},{25,1},{2,10},{10... | collective-permute-start | bytes 245768 | tf_op jit(solution)/shard_map/ppermute | solution.py:113
  23.5 13.6 %collective-permute-start.8 = (f32[5,2,32,128]{3,2,1,0:T(8,128)S(1)}, f32[5,2,32,128]{3,2,1,0:T(8,128)S(1)}, u32[]{:S(2)}, u32[]{:S(2)}) collective-permute-start(f32[5,2,32,128]{3,2,1,0:T(8,128)S(1)} %get-tuple-element.21), channel_id=1, source_target_pairs={{0,24},{8,0},{16,8},{24,16},{1,25},{9,1},{17,9},{25,17},{2,26},{10... | collective-permute-start | bytes 491528 | tf_op jit(solution)/shard_map/ppermute | solution.py:113
  25.6 16.2 %collective-permute-start.6 = (f32[5,2,32,128]{3,2,1,0:T(8,128)S(1)}, f32[5,2,32,128]{3,2,1,0:T(8,128)S(1)}, u32[]{:S(2)}, u32[]{:S(2)}) collective-permute-start(f32[5,2,32,128]{3,2,1,0:T(8,128)S(1)} %get-tuple-element.22), channel_id=1, source_target_pairs={{0,8},{8,16},{16,24},{24,0},{1,9},{9,17},{17,25},{25,1},{2,10},{10... | collective-permute-start | bytes 491528 | tf_op jit(solution)/shard_map/ppermute | solution.py:113
  25.6 19.2 %collective-permute-start.7 = (f32[5,2,32,128]{3,2,1,0:T(8,128)S(1)}, f32[5,2,32,128]{3,2,1,0:T(8,128)S(1)}, u32[]{:S(2)}, u32[]{:S(2)}) collective-permute-start(f32[5,2,32,128]{3,2,1,0:T(8,128)S(1)} %get-tuple-element.24), channel_id=1, source_target_pairs={{0,16},{8,24},{16,0},{24,8},{1,17},{9,25},{17,1},{25,9},{2,18},{10... | collective-permute-start | bytes 491528 | tf_op jit(solution)/shard_map/ppermute | solution.py:113
  30.2 4.4 %collective-permute-start.3 = (f32[5,1,32,128]{3,2,1,0:T(8,128)}, f32[5,1,32,128]{3,2,1,0:T(8,128)S(1)}, u32[]{:S(2)}, u32[]{:S(2)}) collective-permute-start(f32[5,1,32,128]{3,2,1,0:T(8,128)} %get-tuple-element.14), channel_id=1, source_target_pairs={{0,8},{8,16},{16,24},{24,0},{1,9},{9,17},{17,25},{25,1},{2,10},{10... | collective-permute-start | bytes 245768 | tf_op jit(solution)/shard_map/ppermute | solution.py:113
  31.6 18.3 %collective-permute-start.4 = (f32[5,1,32,128]{3,2,1,0:T(8,128)}, f32[5,1,32,128]{3,2,1,0:T(8,128)S(1)}, u32[]{:S(2)}, u32[]{:S(2)}) collective-permute-start(f32[5,1,32,128]{3,2,1,0:T(8,128)} %get-tuple-element.15), channel_id=1, source_target_pairs={{0,16},{8,24},{16,0},{24,8},{1,17},{9,25},{17,1},{25,9},{2,18},{10... | collective-permute-start | bytes 245768 | tf_op jit(solution)/shard_map/ppermute | solution.py:113
  34.6 15.2 %copy-start.6 = (f32[5,1,32,128]{3,2,1,0:T(8,128)}, f32[5,1,32,128]{3,2,1,0:T(8,128)S(1)}, u32[]{:S(2)}) copy-start(f32[5,1,32,128]{3,2,1,0:T(8,128)S(1)} %collective-permute-done.3.refs_1_) | copy-start | bytes 245764
  34.6 15.5 %collective-permute-start.5 = (f32[5,1,32,128]{3,2,1,0:T(8,128)}, f32[5,1,32,128]{3,2,1,0:T(8,128)S(1)}, u32[]{:S(2)}, u32[]{:S(2)}) collective-permute-start(f32[5,1,32,128]{3,2,1,0:T(8,128)} %get-tuple-element.16), channel_id=1, source_target_pairs={{0,24},{8,0},{16,8},{24,16},{1,25},{9,1},{17,9},{25,17},{2,26},{10... | collective-permute-start | bytes 245768 | tf_op jit(solution)/shard_map/ppermute | solution.py:113
  37.1 7.8 %copy-start.3 = (f32[5,2,32,128]{3,2,1,0:T(8,128)}, f32[5,2,32,128]{3,2,1,0:T(8,128)S(1)}, u32[]{:S(2)}) copy-start(f32[5,2,32,128]{3,2,1,0:T(8,128)S(1)} %collective-permute-done.8.refs_3_) | copy-start | bytes 491524
  37.1 15.4 %collective-permute-start.12 = (f32[5,1,32,128]{3,2,1,0:T(8,128)}, f32[5,1,32,128]{3,2,1,0:T(8,128)S(1)}, u32[]{:S(2)}, u32[]{:S(2)}) collective-permute-start(f32[5,1,32,128]{3,2,1,0:T(8,128)} %get-tuple-element.13.refs_0_), channel_id=1, source_target_pairs={{1,0},{2,1},{3,2},{4,3},{5,4},{6,5},{7,6},{9,8},{10,9},{11,10},{12... | collective-permute-start | bytes 245768 | tf_op jit(solution)/shard_map/ppermute | solution.py:151
  41.7 15.2 %collective-permute-start.13 = (f32[5,1,32,128]{3,2,1,0:T(8,128)S(1)}, f32[5,1,32,128]{3,2,1,0:T(8,128)S(1)}, u32[]{:S(2)}, u32[]{:S(2)}) collective-permute-start(f32[5,1,32,128]{3,2,1,0:T(8,128)S(1)} %collective-permute-done.3.refs_1_), channel_id=1, source_target_pairs={{0,1},{1,2},{2,3},{3,4},{4,5},{5,6},{6,7},{9,8},{10,9},{11,10},{12... | collective-permute-start | bytes 245768 | tf_op jit(solution)/shard_map/ppermute | solution.py:151
  49.8 12.9 %collective-permute-start.9 = (f32[5,2,32,128]{3,2,1,0:T(8,128)}, f32[5,2,32,128]{3,2,1,0:T(8,128)S(1)}, u32[]{:S(2)}, u32[]{:S(2)}) collective-permute-start(f32[5,2,32,128]{3,2,1,0:T(8,128)} %get-tuple-element.18), channel_id=1, source_target_pairs={{0,8},{8,16},{16,24},{24,0},{1,9},{9,17},{17,25},{25,1},{2,10},{10... | collective-permute-start | bytes 491528 | tf_op jit(solution)/shard_map/ppermute | solution.py:113
  49.8 13.8 %copy-start.7 = (f32[5,1,32,128]{3,2,1,0:T(8,128)}, f32[5,1,32,128]{3,2,1,0:T(8,128)S(1)}, u32[]{:S(2)}) copy-start(f32[5,1,32,128]{3,2,1,0:T(8,128)S(1)} %collective-permute-done.4.refs_2_) | copy-start | bytes 245764
  49.9 9.0 %copy-start.16 = (f32[96,32]{0,1:T(8,128)S(1)}, f32[96,32]{0,1:T(8,128)}, u32[]{:S(2)}) copy-start(f32[96,32]{0,1:T(8,128)} %param.15) | copy-start | bytes 36868
  49.9 12.8 %collective-permute-start.10 = (f32[5,2,32,128]{3,2,1,0:T(8,128)}, f32[5,2,32,128]{3,2,1,0:T(8,128)S(1)}, u32[]{:S(2)}, u32[]{:S(2)}) collective-permute-start(f32[5,2,32,128]{3,2,1,0:T(8,128)} %get-tuple-element.19), channel_id=1, source_target_pairs={{0,16},{8,24},{16,0},{24,8},{1,17},{9,25},{17,1},{25,9},{2,18},{10... | collective-permute-start | bytes 491528 | tf_op jit(solution)/shard_map/ppermute | solution.py:113
  50.2 13.4 %copy-start.8 = (f32[5,1,32,128]{3,2,1,0:T(8,128)}, f32[5,1,32,128]{3,2,1,0:T(8,128)S(1)}, u32[]{:S(2)}) copy-start(f32[5,1,32,128]{3,2,1,0:T(8,128)S(1)} %collective-permute-done.5.refs_3_) | copy-start | bytes 245764
  50.2 12.6 %collective-permute-start.11 = (f32[5,2,32,128]{3,2,1,0:T(8,128)}, f32[5,2,32,128]{3,2,1,0:T(8,128)S(1)}, u32[]{:S(2)}, u32[]{:S(2)}) collective-permute-start(f32[5,2,32,128]{3,2,1,0:T(8,128)} %get-tuple-element.20), channel_id=1, source_target_pairs={{0,24},{8,0},{16,8},{24,16},{1,25},{9,1},{17,9},{25,17},{2,26},{10... | collective-permute-start | bytes 491528 | tf_op jit(solution)/shard_map/ppermute | solution.py:113
  52.4 11.2 %copy-start.9 = (f32[5,1,32,128]{3,2,1,0:T(8,128)}, f32[5,1,32,128]{3,2,1,0:T(8,128)S(1)}, u32[]{:S(2)}) copy-start(f32[5,1,32,128]{3,2,1,0:T(8,128)S(1)} %collective-permute-done.12.refs_8_) | copy-start | bytes 245764
  52.4 6.6 %collective-permute-start.14 = (f32[5,1,32,128]{3,2,1,0:T(8,128)S(1)}, f32[5,1,32,128]{3,2,1,0:T(8,128)S(1)}, u32[]{:S(2)}, u32[]{:S(2)}) collective-permute-start(f32[5,1,32,128]{3,2,1,0:T(8,128)S(1)} %collective-permute-done.4.refs_2_), channel_id=1, source_target_pairs={{0,1},{1,2},{2,3},{3,4},{4,5},{5,6},{6,7},{8,9},{9,10},{10,11},{11... | collective-permute-start | bytes 245768 | tf_op jit(solution)/shard_map/ppermute | solution.py:151
  56.9 6.7 %copy-start.10 = (f32[5,1,32,128]{3,2,1,0:T(8,128)}, f32[5,1,32,128]{3,2,1,0:T(8,128)S(1)}, u32[]{:S(2)}) copy-start(f32[5,1,32,128]{3,2,1,0:T(8,128)S(1)} %collective-permute-done.13.refs_9_) | copy-start | bytes 245764
  56.9 5.8 %collective-permute-start.15 = (f32[5,1,32,128]{3,2,1,0:T(8,128)S(1)}, f32[5,1,32,128]{3,2,1,0:T(8,128)S(1)}, u32[]{:S(2)}, u32[]{:S(2)}) collective-permute-start(f32[5,1,32,128]{3,2,1,0:T(8,128)S(1)} %collective-permute-done.5.refs_3_), channel_id=1, source_target_pairs={{1,0},{2,1},{3,2},{4,3},{5,4},{6,5},{7,6},{8,9},{9,10},{10,11},{11... | collective-permute-start | bytes 245768 | tf_op jit(solution)/shard_map/ppermute | solution.py:151
  59.1 4.6 %copy-start.11 = (f32[5,1,32,128]{3,2,1,0:T(8,128)}, f32[5,1,32,128]{3,2,1,0:T(8,128)S(1)}, u32[]{:S(2)}) copy-start(f32[5,1,32,128]{3,2,1,0:T(8,128)S(1)} %collective-permute-done.14.refs_10_) | copy-start | bytes 245764
  (11 other events, 11.4 us)
